TPU v7x, 256 devices: a 2x2x32 block of a 4x8x32 slice. The times are simulated.
256 devices in a mesh: groups: 4 (over x, y), ep: 32 (over z), node: 2 (over core).
Axes of the slice: x: 2, y: 2, z: 32, core: 2. Of those that a mesh axis runs over, the one named last changes fastest.
The devices are a block of a 4x8x32 slice.
Arguments:
- tokens: bfloat16 [8192, 7168], P(('groups', 'ep', 'node')), parts along dimension 0, may hold values from -6 to 6
- expert_ids: int32 [8192, 8], P(('groups', 'ep', 'node')), parts along dimension 0, may hold values from 0 to 63, all different within a row; in each aligned block of 32 rows (0 to 31, 32 to 63, ...) at most 8 rows name the same one
- gate_weights: float32 [8192, 8], P(('groups', 'ep', 'node')), parts along dimension 0, may hold values from 0.05 to 0.5
- gate_up_weight: bfloat16 [64, 7168, 512], P(('ep', 'node')), may hold values from -0.0625 to 0.0625
- down_weight: bfloat16 [64, 256, 7168], P(('ep', 'node')), may hold values from -0.375 to 0.375
Outputs:
- moe_out: bfloat16 [8192, 7168], P(('groups', 'ep', 'node')), parts along dimension 0
There are 4 independent parts, one for each index of `groups`. A program takes and returns all parts, laid end to end along the dimension named above; an argument that names none is the same for every part. Nothing has to cross between parts.
Inputs may be any that keep to these rules, and one draw needn't show every extreme that they name: `expert_ids`: each token names 8 different experts; among the 32 tokens of one device no expert is named by more than 8 of them, a bound that some block reaches.
All inputs are finite; a program needn't handle non-finite values.
Results may differ from a plain program's by a relative error of at most 0.0058.
Values may be sent and summed in bfloat16 or wider, within the bound.
A program may use at most 128 MiB of HBM per device.

v0:
```python
import jax
import jax.numpy as jnp
from jax import lax
from jax.sharding import PartitionSpec as P


def run_experts(received, gate_up_weight, down_weight):
    inner_width = down_weight.shape[1]
    slot_rows = received[:, 0].reshape(-1, received.shape[3])
    gate_up = jnp.dot(slot_rows, gate_up_weight[0], preferred_element_type=jnp.float32)
    hidden = (jax.nn.silu(gate_up[:, :inner_width]) * gate_up[:, inner_width:]).astype(jnp.bfloat16)
    product = jnp.dot(hidden, down_weight[0], preferred_element_type=jnp.float32).astype(
        jnp.bfloat16
    )
    results = [product.reshape(received.shape[0], received.shape[2], received.shape[3])]
    return jnp.stack(results, axis=1)


def on_device(tokens, expert_ids, gate_weights, gate_up_weight, down_weight):
    ep_size = lax.axis_size("ep")
    node_size = lax.axis_size("node")
    devices = ep_size * node_size
    local_count = gate_up_weight.shape[0]
    expert_total = devices * local_count
    token_count = tokens.shape[0]
    model_width = tokens.shape[1]
    top_count = expert_ids.shape[1]
    capacity = max(2, (2 * token_count * top_count + expert_total - 1) // expert_total)
    flat_ids = expert_ids.reshape(-1)
    one_hot = (flat_ids[:, None] == jnp.arange(expert_total, dtype=jnp.int32)[None, :]).astype(
        jnp.int32
    )
    slot_rank = jnp.sum(jnp.cumsum(one_hot, axis=0) * one_hot, axis=1) - 1
    slot_index = flat_ids * capacity + slot_rank
    sources = jnp.arange(token_count * top_count, dtype=jnp.int32) // top_count
    outgoing = (
        jnp.zeros((expert_total * capacity, model_width), jnp.bfloat16)
        .at[slot_index]
        .set(tokens[sources])
    )
    outgoing = outgoing.reshape(devices, local_count, capacity, model_width)
    answers = run_experts(
        lax.all_to_all(outgoing, ("ep", "node"), split_axis=0, concat_axis=0, tiled=True),
        gate_up_weight,
        down_weight,
    )
    returned = lax.all_to_all(answers, ("ep", "node"), split_axis=0, concat_axis=0, tiled=True)
    returned = returned.reshape(expert_total * capacity, model_width)
    picked = returned[slot_index].astype(jnp.float32).reshape(token_count, top_count, model_width)
    combined = jnp.sum(gate_weights[:, :, None] * picked, axis=1).astype(jnp.bfloat16)
    return combined


def solution(mesh):
    placed = (
        P(("groups", "ep", "node"), None),
        P(("groups", "ep", "node"), None),
        P(("groups", "ep", "node"), None),
        P(("ep", "node"), None, None),
        P(("ep", "node"), None, None),
    )
    return jax.shard_map(
        on_device,
        mesh=mesh,
        in_specs=placed,
        out_specs=P(("groups", "ep", "node"), None),
        check_vma=False,
    )
```

profile of v0, /device:TPU:37, one launch (start us, length us, event | category | flops | bytes accessed | tf_op | source)
XLA Modules:
  0.0 1379.5 jit_solution(9172816720959031247)
XLA Ops:
  0.0 0.0 copy-start
  0.0 0.8 copy.14
  0.8 0.1 eq.29
  0.9 0.1 eq.25
  1.0 0.7 broadcast_multiply_fusion
  1.7 0.6 reduce-window.6
  2.3 0.2 slice_reduce_fusion
  2.6 0.1 fusion.13
  2.7 0.1 copy.13
  2.8 0.1 mul.37
  2.9 0.0 copy-done
  2.9 20.4 %scatter_custom_fusion = bf16[512,7168]{1,0:T(8,128)(2,1)} fusion(s32[256]{0:T(256)S(1)} %bitcast.37, bf16[32,7168]{1,0:T(8,128)(2,1)S(1)} %copy-done, s32[1024]{0:T(1024)S(1)} %pad_clamp_fusion.1, bf16[]{:T(256)} %constant.28.clone.1), kind=kCustom, calls=%fused_computation.11 | custom fusion | bytes 7340034 | tf_op jit(solution)/shard_map/scatter | solution.py:39
  23.3 681.4 %all_to_all.10 = bf16[64,1,8,7168]{3,2,1,0:T(8,128)(2,1)S(1)} all-to-all(bf16[64,1,8,7168]{3,2,1,0:T(8,128)(2,1)} %bitcast.36), channel_id=1, replica_groups=mesh['groups'=4,'ep'=32,'node'=2] {'ep','node'}, dimensions={0} | all-to-all | bytes 14680064 | tf_op jit(solution)/shard_map/all_to_all | solution.py:43
  704.7 0.0 copy-start.1
  704.7 6.5 fusion.2
  711.2 0.0 copy-done.1
  711.2 5.2 fusion
  716.3 0.0 copy-start.2
  716.3 9.2 all-to-all-start.1
  725.5 0.0 copy-done.2
  725.5 0.1 copy.12
  725.6 636.2 %all-to-all-done.1 = bf16[64,1,8,7168]{3,2,1,0:T(8,128)(2,1)} async-done(((bf16[64,1,8,7168]{3,2,1,0:T(8,128)(2,1)}), bf16[64,1,8,7168]{3,2,1,0:T(8,128)(2,1)}, u32[]{:S(2)}, u32[]{:S(2)}) %all-to-all-start.1) | async-done | bytes 7340064 | tf_op jit(solution)/shard_map/all_to_all | solution.py:47
  1361.8 12.1 gather_fusion
  1373.9 5.4 fusion.1
  (8 shorter events, 0.1 us)
Async XLA Ops:
  0.0 2.9 copy-start
  704.7 6.5 copy-start.1
  716.3 9.2 copy-start.2
  716.3 645.4 %all-to-all-start.1 = ((bf16[64,1,8,7168]{3,2,1,0:T(8,128)(2,1)}), bf16[64,1,8,7168]{3,2,1,0:T(8,128)(2,1)}, u32[]{:S(2)}, u32[]{:S(2)}) async-start(bf16[64,1,8,7168]{3,2,1,0:T(8,128)(2,1)} %fusion), calls=%async_computation.1 | async-start | bytes 14680064 | tf_op jit(solution)/shard_map/all_to_all | solution.py:47
where the time goes:
time: 1410 us; the launch traced here: 1380 us
  blocking collectives  681 us (48%)
  waiting for transfers between devices  636 us (45%)
  local copies, waits for them, and re-layouts  34 us (2%)
    all_to_all x1, blocking collectives, on_device(): lax.all_to_all(outgoing, ('ep', 'node'), split_axis=0, concat_axis=0, til...  681 us
    all_to_all x1, waiting for transfers between devices, on_device(): lax.all_to_all(answers, ('ep', 'node'), split_axis=0, concat_axis=0, tile...  636 us
  transfers between devices with their start and end apart: 1, of which 1 were waited for; matrix products, arithmetic and copies ran while one was open for 0% of the time, Pallas kernels for 0%

commit v1 on v0

v1 whole, which is shorter than its diff:
```python
import functools

import jax
import jax.numpy as jnp
from jax import lax
from jax.experimental import pallas as pl
from jax.experimental.pallas import tpu as pltpu
from jax.sharding import PartitionSpec as P

MESH = pl.DeviceIdType.MESH
BF16 = jnp.bfloat16
F32 = jnp.float32
LEFT, RIGHT = 0, 1


def moe_kernel(
    n, nch, top,
    tok_hbm, meta_in, gu_hbm, dn_hbm, out_ref,
    tok, meta, wgu, wd, hid, acc, part,
    load_sem, w_send, w_recv, ag_send, ag_recv, meta_send, meta_recv, rs_send, rs_recv,
):
    half = n // 2
    hch = nch // 2
    rows, width = tok.shape[2], tok.shape[3]
    inner = dn_hbm.shape[1]
    me = lax.axis_index("ep")
    core = lax.axis_index("node")
    right, left = lax.rem(me + 1, n), lax.rem(me + n - 1, n)
    peer = 1 - core

    barrier = pltpu.get_barrier_semaphore()
    pl.semaphore_signal(barrier, inc=1, device_id={"ep": left}, device_id_type=MESH)
    pl.semaphore_signal(barrier, inc=1, device_id={"ep": right}, device_id_type=MESH)
    pl.semaphore_signal(barrier, inc=1, device_id={"node": peer}, device_id_type=MESH)

    loads = []
    for j in range(nch):
        loads.append(pltpu.make_async_copy(
            tok_hbm.at[:, pl.ds(j * width, width)], tok.at[0, j], load_sem.at[j]))
    loads.append(pltpu.make_async_copy(meta_in, meta.at[0], load_sem.at[nch]))
    for c in loads:
        c.start()
    w_loads = [pltpu.make_async_copy(gu_hbm.at[0], wgu.at[0], load_sem.at[nch + 1])]
    w_remote = [pltpu.make_async_remote_copy(
        src_ref=gu_hbm.at[0], dst_ref=wgu.at[1], send_sem=w_send.at[0], recv_sem=w_recv.at[0],
        device_id={"node": peer}, device_id_type=MESH)]
    for j in range(nch):
        src = dn_hbm.at[0, :, pl.ds(j * width, width)]
        w_loads.append(pltpu.make_async_copy(
            src, wd.at[j, pl.ds(0, inner)], load_sem.at[nch + 2 + j]))
        w_remote.append(pltpu.make_async_remote_copy(
            src_ref=src, dst_ref=wd.at[j, pl.ds(inner, inner)],
            send_sem=w_send.at[1 + j], recv_sem=w_recv.at[1 + j],
            device_id={"node": peer}, device_id_type=MESH))
    for c in loads:
        c.wait()
    for c in w_loads:
        c.start()
    pl.semaphore_wait(barrier, 3)

    def slots(direction, s):
        return lax.rem(n - s, n) if direction == LEFT else s

    def ag(direction, s, j):
        return pltpu.make_async_remote_copy(
            src_ref=tok.at[slots(direction, s - 1), j], dst_ref=tok.at[slots(direction, s), j],
            send_sem=ag_send.at[direction, j], recv_sem=ag_recv.at[direction, s, j],
            device_id={"ep": left if direction == LEFT else right}, device_id_type=MESH)

    def ag_meta(direction, s):
        return pltpu.make_async_remote_copy(
            src_ref=meta.at[slots(direction, s - 1)], dst_ref=meta.at[slots(direction, s)],
            send_sem=meta_send.at[direction], recv_sem=meta_recv.at[direction, s],
            device_id={"ep": left if direction == LEFT else right}, device_id_type=MESH)

    def rs(direction, d, j):
        return pltpu.make_async_remote_copy(
            src_ref=part.at[direction, d, j], dst_ref=part.at[direction, d - 1, j],
            send_sem=rs_send.at[direction, j], recv_sem=rs_recv.at[direction, d - 1, j],
            device_id={"ep": left if direction == LEFT else right}, device_id_type=MESH)

    def rs_arrive(direction, d, j):
        return rs(direction, d + 1, j)

    def loop(lo, hi, body):
        def step(i, carry):
            body(i)
            return carry
        lax.fori_loop(lo, hi, step, 0)

    def matmul(a, b, j):
        x = jnp.concatenate([tok[a, j], tok[b, j]], axis=0)
        for e in range(2):
            at = pl.ds(e * 2 * inner, 2 * inner)
            w = wgu[e, pl.ds(pl.multiple_of(j * width, width), width), :]
            acc[:, at] += jnp.dot(x, w, preferred_element_type=F32)

    same = (lax.broadcasted_iota(jnp.int32, (rows, 128), 0)
            == lax.broadcasted_iota(jnp.int32, (rows, 128), 1))

    def gate_column(slot, expert):
        ids = meta[slot]
        gates = pltpu.roll(ids, 128 - rows, 1)
        row = jnp.sum(jnp.where(ids == expert, gates, 0.0), axis=0, keepdims=True)
        return jnp.sum(jnp.where(same, row, 0.0), axis=1, keepdims=True)

    def activate(a, b):
        for e, owner in ((0, core), (1, peer)):
            expert = (me * 2 + owner).astype(F32)
            g = jnp.concatenate([gate_column(a, expert), gate_column(b, expert)], axis=0)
            gate = acc[:, pl.ds(e * 2 * inner, inner)]
            up = acc[:, pl.ds(e * 2 * inner + inner, inner)]
            h = (gate * (1.0 / (1.0 + jnp.exp(-gate))) * up * g).astype(BF16)
            hid[a, :, pl.ds(e * inner, inner)] = h[:rows]
            hid[b, :, pl.ds(e * inner, inner)] = h[rows:]
        acc[...] = jnp.zeros_like(acc)

    for j in range(nch):
        for direction in (LEFT, RIGHT):
            ag(direction, 1, j).start()
    for direction in (LEFT, RIGHT):
        ag_meta(direction, 1).start()
    for c in w_remote:
        c.start()
    acc[...] = jnp.zeros_like(acc)

    def pass_on(s, j, directions):
        for direction in (LEFT, RIGHT):
            arrived = ag(direction, s, j)
            arrived.wait_recv()
            arrived.wait_send()
            if direction in directions:
                ag(direction, s + 1, j).start()

    def pass_meta(s, directions):
        for direction in (LEFT, RIGHT):
            arrived = ag_meta(direction, s)
            arrived.wait_recv()
            arrived.wait_send()
            if direction in directions:
                ag_meta(direction, s + 1).start()

    loop(0, nch, lambda j: pass_on(1, j, (LEFT, RIGHT)))
    pass_meta(1, (LEFT, RIGHT))
    w_loads[0].wait()
    w_remote[0].wait_recv()

    def gather_step(s):
        def chunk(j):
            pass_on(s, j, (LEFT, RIGHT))
            matmul(s - 1, n - s + 1, j)
        loop(0, nch, chunk)
        pass_meta(s, (LEFT, RIGHT))
        activate(s - 1, n - s + 1)

    loop(2, half - 1, gather_step)

    def last_right(j):
        pass_on(half - 1, j, (RIGHT,))
        matmul(half - 2, half + 2, j)

    def last_left(j):
        pass_on(half - 1, j, (LEFT,))
        matmul(half - 2, half + 2, j)

    loop(0, hch, last_right)
    loop(hch, nch, last_left)
    pass_meta(half - 1, (RIGHT,))
    activate(half - 2, half + 2)

    loop(0, nch, lambda j: matmul(half - 1, half + 1, j))
    activate(half - 1, half + 1)

    for c in w_loads[1:]:
        c.wait()
    for c in w_remote[1:]:
        c.wait_recv()

    def pair(d, j):
        h = jnp.concatenate([hid[d], hid[n - d]], axis=0)
        return jnp.dot(h, wd[j], preferred_element_type=F32)

    def free_chunk(direction):
        def body(j):
            h = hid[half - 1] if direction == LEFT else hid[half + 1]
            part[direction, half - 1, j] = jnp.dot(
                h, wd[j], preferred_element_type=F32).astype(BF16)
            rs(direction, half - 1, j).start()
        return body

    loop(hch, nch, free_chunk(LEFT))
    loop(0, hch, free_chunk(RIGHT))

    def far(direction):
        def body(j):
            ag(direction, half, j).wait_recv()
            ag(direction, half, j).wait_send()
            matmul(half, 0, j)
        return body

    loop(0, hch, far(RIGHT))
    loop(hch, nch, far(LEFT))
    ag_meta(RIGHT, half).wait()
    activate(half, 0)

    def far_chunk(direction):
        def body(j):
            part[direction, half, j] = jnp.dot(
                hid[half], wd[j], preferred_element_type=F32).astype(BF16)
            rs(direction, half, j).start()
        return body

    loop(0, hch, far_chunk(LEFT))
    loop(hch, nch, far_chunk(RIGHT))

    def second_chunk(direction):
        def body(j):
            h = hid[half - 1] if direction == LEFT else hid[half + 1]
            mine = jnp.dot(h, wd[j], preferred_element_type=F32)
            rs_arrive(direction, half - 1, j).wait_recv()
            total = mine + part[direction, half - 1, j].astype(F32)
            part[direction, half - 1, j] = total.astype(BF16)
            rs(direction, half, j).wait_send()
            rs(direction, half - 1, j).start()
        return body

    loop(0, hch, second_chunk(LEFT))
    loop(hch, nch, second_chunk(RIGHT))

    def reduce_step(i):
        d = half - 2 - i

        def chunk(j):
            mine = pair(d, j)
            for direction in (LEFT, RIGHT):
                rs_arrive(direction, d, j).wait_recv()
                own = mine[:rows] if direction == LEFT else mine[rows:]
                total = own + part[direction, d, j].astype(F32)
                part[direction, d, j] = total.astype(BF16)
                rs(direction, d + 1, j).wait_send()
            for direction in (LEFT, RIGHT):
                rs(direction, d, j).start()
        loop(0, nch, chunk)

    loop(0, half - 2, reduce_step)

    for j in range(nch):
        total = jnp.dot(hid[0], wd[j], preferred_element_type=F32)
        for direction in (LEFT, RIGHT):
            rs_arrive(direction, 0, j).wait()
            total = total + part[direction, 0, j].astype(F32)
        out_ref[:, pl.ds(j * width, width)] = total.astype(BF16)
    for c in w_remote:
        c.wait_send()


def on_device(n, tokens, expert_ids, gate_weights, gate_up_weight, down_weight):
    rows, model = tokens.shape
    top = expert_ids.shape[1]
    inner = down_weight.shape[1]
    nch = 4
    width = model // nch
    half = n // 2
    meta = jnp.concatenate(
        [expert_ids.T.astype(F32), gate_weights.T, jnp.zeros((top, 128 - 2 * rows), F32)], axis=1)
    dma = pltpu.SemaphoreType.DMA
    hbm = pl.BlockSpec(memory_space=pl.ANY)
    vmem = pl.BlockSpec(memory_space=pltpu.VMEM)
    return pl.pallas_call(
        functools.partial(moe_kernel, n, nch, top),
        out_shape=jax.ShapeDtypeStruct((rows, model), BF16),
        in_specs=[hbm, vmem, hbm, hbm],
        out_specs=vmem,
        scratch_shapes=[
            pltpu.VMEM((n, nch, rows, width), BF16),
            pltpu.VMEM((n, top, 128), F32),
            pltpu.VMEM((2, model, 2 * inner), BF16),
            pltpu.VMEM((nch, 2 * inner, width), BF16),
            pltpu.VMEM((n, rows, 2 * inner), BF16),
            pltpu.VMEM((2 * rows, 4 * inner), F32),
            pltpu.VMEM((2, half + 1, nch, rows, width), BF16),
            dma((2 * nch + 2,)),
            dma((1 + nch,)),
            dma((1 + nch,)),
            dma((2, nch)),
            dma((2, half + 1, nch)),
            dma((2,)),
            dma((2, half + 1)),
            dma((2, nch)),
            dma((2, half + 1, nch)),
        ],
        compiler_params=pltpu.CompilerParams(
            collective_id=0, has_side_effects=True, vmem_limit_bytes=66_000_000),
        name="moe_ring",
    )(tokens, meta, gate_up_weight, down_weight)


def solution(mesh):
    placed = (
        P(("groups", "ep", "node"), None),
        P(("groups", "ep", "node"), None),
        P(("groups", "ep", "node"), None),
        P(("ep", "node"), None, None),
        P(("ep", "node"), None, None),
    )
    return jax.shard_map(
        functools.partial(on_device, mesh.shape["ep"]),
        mesh=mesh,
        in_specs=placed,
        out_specs=P(("groups", "ep", "node"), None),
        check_vma=False,
    )
```

time: 1410 us -> 343 us (0.24); the launches traced: 1380 us -> 339 us
  blocking collectives: 681 us -> 0 us
  waiting for transfers between devices: 636 us -> 0 us
  Pallas kernels: 0 us -> 335 us
  local copies, waits for them, and re-layouts: 34 us -> 1.89 us
    all_to_all x1 -> x0, blocking collectives: 681 us -> none  [on_device(): lax.all_to_all(outgoing, ('ep', 'node'), split_axis=0, concat_axis=0, til...]
    all_to_all x1 -> x0, waiting for transfers between devices: 636 us -> none  [on_device(): lax.all_to_all(answers, ('ep', 'node'), split_axis=0, concat_axis=0, tile...]
    pallas_call x0 -> x1, Pallas kernels: none -> 335 us  [on_device(): pl.pallas_call(functools.partial(moe_kernel, n, nch, top), out_shape=jax....]
    scatter x1 -> x0, local copies, waits for them, and re-layouts: 20.4 us -> none  [on_device(): outgoing = jnp.zeros((expert_total * capacity, model_width), jnp.bfloat16...]
  transfers between devices with their start and end apart: 1 -> 0, of which waited for: 1 -> 0; matrix products, arithmetic and copies ran while one was open for 0% -> 0% of each run, Pallas kernels for 0% -> 0%
where the time goes in v1:
time: 343 us; the launch traced here: 339 us
  Pallas kernels  335 us (98%)
    pallas_call x1, Pallas kernels, on_device(): pl.pallas_call(functools.partial(moe_kernel, n, nch, top), out_shape=jax....  335 us

profile of v1, /device:TPU:37, one launch (start us, length us, event | category | flops | bytes accessed | tf_op | source)
XLA Modules:
  0.0 338.9 jit_solution(10426320987481546146)
XLA Ops:
  0.0 0.1 pad.2.clone
  0.1 0.7 convert_bitcast_fusion
  0.8 1.4 maximum_maximum_fusion.meta_in
  2.1 335.0 %moe_ring.1 = bf16[32,7168]{1,0:T(8,128)(2,1)} custom-call(bf16[32,7168]{1,0:T(8,128)(2,1)} %tok_hbm.1, f32[8,128]{1,0:T(8,128)} %maximum_maximum_fusion.meta_in, bf16[1,7168,512]{2,1,0:T(8,128)(2,1)} %gu_hbm.1, bf16[1,256,7168]{2,1,0:T(8,128)(2,1)} %dn_hbm.1), custom_call_target="tpu_custom_call" | custom-call | tf_op jit(solution)/shard_map/moe_ring/pallas_call | solution.py:269
  337.1 1.8 copy.7
  (1 shorter events, 0.0 us)

commit v2 on v1

v2 whole, which is shorter than its diff:
```python
import functools

import jax
import jax.numpy as jnp
from jax import lax
from jax.experimental import pallas as pl
from jax.experimental.pallas import tpu as pltpu
from jax.sharding import PartitionSpec as P

MESH = pl.DeviceIdType.MESH
BF16 = jnp.bfloat16
F32 = jnp.float32
LEFT, RIGHT = 0, 1


def moe_kernel(
    n, nch, top,
    tok_hbm, ids_hbm, gates_hbm, gu_hbm, dn_hbm, out_hbm,
    tok, ids_in, gates_in, meta, wgu, wd, hid, acc, part, out_buf,
    load_sem, out_sem, w_send, w_recv, ag_send, ag_recv, meta_send, meta_recv, rs_send, rs_recv,
):
    half = n // 2
    hch = nch // 2
    rows, width = tok.shape[2], tok.shape[3]
    inner = dn_hbm.shape[1]
    me = lax.axis_index("ep")
    core = lax.axis_index("node")
    right, left = lax.rem(me + 1, n), lax.rem(me + n - 1, n)
    peer = 1 - core

    barrier = pltpu.get_barrier_semaphore()
    pl.semaphore_signal(barrier, inc=1, device_id={"ep": left}, device_id_type=MESH)
    pl.semaphore_signal(barrier, inc=1, device_id={"ep": right}, device_id_type=MESH)
    pl.semaphore_signal(barrier, inc=1, device_id={"node": peer}, device_id_type=MESH)

    tok_loads = [pltpu.make_async_copy(
        tok_hbm.at[:, pl.ds(j * width, width)], tok.at[0, j], load_sem.at[j]) for j in range(nch)]
    meta_loads = [
        pltpu.make_async_copy(ids_hbm, ids_in, load_sem.at[nch]),
        pltpu.make_async_copy(gates_hbm, gates_in, load_sem.at[nch + 1]),
    ]
    for c in tok_loads + meta_loads:
        c.start()

    def gu_load(j):
        at = pl.ds(j * width, width)
        return pltpu.make_async_copy(gu_hbm.at[0, at], wgu.at[0, at], load_sem.at[nch + 2 + j])

    def gu_swap(j):
        at = pl.ds(j * width, width)
        return pltpu.make_async_remote_copy(
            src_ref=gu_hbm.at[0, at], dst_ref=wgu.at[1, at],
            send_sem=w_send.at[j], recv_sem=w_recv.at[j],
            device_id={"node": peer}, device_id_type=MESH)

    def dn_load(j):
        return pltpu.make_async_copy(
            dn_hbm.at[0, :, pl.ds(j * width, width)], wd.at[j, pl.ds(0, inner)],
            load_sem.at[2 * nch + 2 + j])

    def dn_swap(j):
        return pltpu.make_async_remote_copy(
            src_ref=dn_hbm.at[0, :, pl.ds(j * width, width)], dst_ref=wd.at[j, pl.ds(inner, inner)],
            send_sem=w_send.at[nch + j], recv_sem=w_recv.at[nch + j],
            device_id={"node": peer}, device_id_type=MESH)

    for c in meta_loads:
        c.wait()
    meta[0] = jnp.concatenate(
        [ids_in[...].astype(F32), gates_in[...], jnp.zeros((top, 128 - 2 * rows), F32)], axis=1)
    pl.semaphore_wait(barrier, 3)

    def slots(direction, s):
        return lax.rem(n - s, n) if direction == LEFT else s

    def ag(direction, s, j):
        return pltpu.make_async_remote_copy(
            src_ref=tok.at[slots(direction, s - 1), j], dst_ref=tok.at[slots(direction, s), j],
            send_sem=ag_send.at[direction, j], recv_sem=ag_recv.at[direction, s, j],
            device_id={"ep": left if direction == LEFT else right}, device_id_type=MESH)

    def ag_meta(direction, s):
        return pltpu.make_async_remote_copy(
            src_ref=meta.at[slots(direction, s - 1)], dst_ref=meta.at[slots(direction, s)],
            send_sem=meta_send.at[direction], recv_sem=meta_recv.at[direction, s],
            device_id={"ep": left if direction == LEFT else right}, device_id_type=MESH)

    def rs(direction, d, j):
        return pltpu.make_async_remote_copy(
            src_ref=part.at[direction, d, j], dst_ref=part.at[direction, d - 1, j],
            send_sem=rs_send.at[direction, j], recv_sem=rs_recv.at[direction, d - 1, j],
            device_id={"ep": left if direction == LEFT else right}, device_id_type=MESH)

    def rs_arrive(direction, d, j):
        return rs(direction, d + 1, j)

    def loop(lo, hi, body):
        def step(i, carry):
            body(i)
            return carry
        lax.fori_loop(lo, hi, step, 0)

    def matmul(blocks, j):
        x = jnp.concatenate([tok[a, j] for a in blocks], axis=0)
        for e in range(2):
            at = pl.ds(e * 2 * inner, 2 * inner)
            w = wgu[e, pl.ds(pl.multiple_of(j * width, width), width), :]
            acc[: len(blocks) * rows, at] += jnp.dot(x, w, preferred_element_type=F32)

    same = (lax.broadcasted_iota(jnp.int32, (rows, 128), 0)
            == lax.broadcasted_iota(jnp.int32, (rows, 128), 1))

    def gate_column(slot, expert):
        ids = meta[slot]
        gates = pltpu.roll(ids, 128 - rows, 1)
        row = jnp.sum(jnp.where(ids == expert, gates, 0.0), axis=0, keepdims=True)
        return jnp.sum(jnp.where(same, row, 0.0), axis=1, keepdims=True)

    def activate(blocks):
        count = len(blocks) * rows
        for e, owner in ((0, core), (1, peer)):
            expert = (me * 2 + owner).astype(F32)
            g = jnp.concatenate([gate_column(a, expert) for a in blocks], axis=0)
            gate = acc[:count, pl.ds(e * 2 * inner, inner)]
            up = acc[:count, pl.ds(e * 2 * inner + inner, inner)]
            h = (gate * (1.0 / (1.0 + jnp.exp(-gate))) * up * g).astype(BF16)
            for i, a in enumerate(blocks):
                hid[a, :, pl.ds(e * inner, inner)] = h[i * rows:(i + 1) * rows]
        acc[:count, :] = jnp.zeros((count, 4 * inner), F32)

    for j in range(nch):
        tok_loads[j].wait()
        for direction in (LEFT, RIGHT):
            ag(direction, 1, j).start()
    for direction in (LEFT, RIGHT):
        ag_meta(direction, 1).start()
    for j in range(nch):
        gu_load(j).start()
        gu_swap(j).start()
    acc[...] = jnp.zeros_like(acc)

    def pass_on(s, j, directions):
        for direction in (LEFT, RIGHT):
            arrived = ag(direction, s, j)
            arrived.wait_recv()
            arrived.wait_send()
            if direction in directions:
                ag(direction, s + 1, j).start()

    def pass_meta(s, directions):
        for direction in (LEFT, RIGHT):
            arrived = ag_meta(direction, s)
            arrived.wait_recv()
            arrived.wait_send()
            if direction in directions:
                ag_meta(direction, s + 1).start()

    loop(0, nch, lambda j: pass_on(1, j, (LEFT, RIGHT)))
    pass_meta(1, (LEFT, RIGHT))

    def first_chunks(j):
        pass_on(2, j, (LEFT, RIGHT))
        gu_load(j).wait()
        gu_swap(j).wait_recv()
        dn_load(j).start()
        dn_swap(j).start()
        matmul((0, 1, n - 1, 2, n - 2), j)

    loop(0, nch, first_chunks)
    pass_meta(2, (LEFT, RIGHT))
    activate((0, 1, n - 1, 2, n - 2))

    def gather_step(s):
        def chunk(j):
            pass_on(s, j, (LEFT, RIGHT))
            matmul((s, n - s), j)
        loop(0, nch, chunk)
        pass_meta(s, (LEFT, RIGHT))
        activate((s, n - s))

    loop(3, half - 1, gather_step)

    def last_right(j):
        pass_on(half - 1, j, (RIGHT,))
        matmul((half - 1, half + 1), j)

    def last_left(j):
        pass_on(half - 1, j, (LEFT,))
        matmul((half - 1, half + 1), j)

    loop(0, hch, last_right)
    loop(hch, nch, last_left)
    pass_meta(half - 1, (RIGHT,))
    for j in range(nch):
        dn_load(j).wait()
        dn_swap(j).wait_recv()
    activate((half - 1, half + 1))

    def pair(d, j):
        h = jnp.concatenate([hid[d], hid[n - d]], axis=0)
        return jnp.dot(h, wd[j], preferred_element_type=F32)

    sides = ((LEFT, half - 1, 0), (RIGHT, half + 1, hch))

    def free_chunk(i):
        for direction, slot, first in sides:
            j = hch - first + i
            part[direction, half - 1, j] = jnp.dot(
                hid[slot], wd[j], preferred_element_type=F32).astype(BF16)
            rs(direction, half - 1, j).start()

    loop(0, hch, free_chunk)

    def far(i):
        for direction, first in ((RIGHT, 0), (LEFT, hch)):
            j = first + i
            ag(direction, half, j).wait()
            matmul((half,), j)

    loop(0, hch, far)
    ag_meta(RIGHT, half).wait()
    activate((half,))

    def far_chunk(i):
        for direction, slot, first in sides:
            j = first + i
            part[direction, half, j] = jnp.dot(
                hid[half], wd[j], preferred_element_type=F32).astype(BF16)
            rs(direction, half, j).start()

    loop(0, hch, far_chunk)

    def second_chunk(i):
        for direction, slot, first in sides:
            j = first + i
            mine = jnp.dot(hid[slot], wd[j], preferred_element_type=F32)
            rs_arrive(direction, half - 1, j).wait_recv()
            total = mine + part[direction, half - 1, j].astype(F32)
            part[direction, half - 1, j] = total.astype(BF16)
            rs(direction, half, j).wait_send()
            rs(direction, half - 1, j).start()

    loop(0, hch, second_chunk)

    def reduce_step(i):
        d = half - 2 - i

        def chunk(j):
            mine = pair(d, j)
            for direction in (LEFT, RIGHT):
                rs_arrive(direction, d, j).wait_recv()
                own = mine[:rows] if direction == LEFT else mine[rows:]
                total = own + part[direction, d, j].astype(F32)
                part[direction, d, j] = total.astype(BF16)
                rs(direction, d + 1, j).wait_send()
            for direction in (LEFT, RIGHT):
                rs(direction, d, j).start()
        loop(0, nch, chunk)

    loop(0, half - 2, reduce_step)

    def out_copy(j):
        return pltpu.make_async_copy(
            out_buf.at[j], out_hbm.at[:, pl.ds(j * width, width)], out_sem.at[j])

    for j in range(nch):
        total = jnp.dot(hid[0], wd[j], preferred_element_type=F32)
        for direction in (LEFT, RIGHT):
            rs_arrive(direction, 0, j).wait()
            total = total + part[direction, 0, j].astype(F32)
        out_buf[j] = total.astype(BF16)
        out_copy(j).start()
    for j in range(nch):
        gu_swap(j).wait_send()
        dn_swap(j).wait_send()
        out_copy(j).wait()


def on_device(n, tokens, expert_ids, gate_weights, gate_up_weight, down_weight):
    rows, model = tokens.shape
    top = expert_ids.shape[1]
    inner = down_weight.shape[1]
    nch = 4
    width = model // nch
    half = n // 2
    dma = pltpu.SemaphoreType.DMA
    hbm = pl.BlockSpec(memory_space=pl.ANY)
    return pl.pallas_call(
        functools.partial(moe_kernel, n, nch, top),
        out_shape=jax.ShapeDtypeStruct((rows, model), BF16),
        in_specs=[hbm] * 5,
        out_specs=hbm,
        scratch_shapes=[
            pltpu.VMEM((n, nch, rows, width), BF16),
            pltpu.VMEM((top, rows), jnp.int32),
            pltpu.VMEM((top, rows), F32),
            pltpu.VMEM((n, top, 128), F32),
            pltpu.VMEM((2, model, 2 * inner), BF16),
            pltpu.VMEM((nch, 2 * inner, width), BF16),
            pltpu.VMEM((n, rows, 2 * inner), BF16),
            pltpu.VMEM((5 * rows, 4 * inner), F32),
            pltpu.VMEM((2, half + 1, nch, rows, width), BF16),
            pltpu.VMEM((nch, rows, width), BF16),
            dma((3 * nch + 2,)),
            dma((nch,)),
            dma((2 * nch,)),
            dma((2 * nch,)),
            dma((2, nch)),
            dma((2, half + 1, nch)),
            dma((2,)),
            dma((2, half + 1)),
            dma((2, nch)),
            dma((2, half + 1, nch)),
        ],
        compiler_params=pltpu.CompilerParams(
            collective_id=0, has_side_effects=True, vmem_limit_bytes=66_000_000),
        name="moe_ring",
    )(tokens, expert_ids.T, gate_weights.T, gate_up_weight, down_weight)


def solution(mesh):
    placed = (
        P(("groups", "ep", "node"), None),
        P(("groups", "ep", "node"), None),
        P(("groups", "ep", "node"), None),
        P(("ep", "node"), None, None),
        P(("ep", "node"), None, None),
    )
    return jax.shard_map(
        functools.partial(on_device, mesh.shape["ep"]),
        mesh=mesh,
        in_specs=placed,
        out_specs=P(("groups", "ep", "node"), None),
        check_vma=False,
    )
```

time: 343 us -> 338 us (0.985); the launches traced: 339 us -> 338 us
  no operation moved by 1% of the time
where the time goes in v2:
time: 338 us
  Pallas kernels  336 us (99%)
    pallas_call x1, Pallas kernels, on_device(): pl.pallas_call(functools.partial(moe_kernel, n, nch, top), out_shape=jax....  336 us

profile of v2, /device:TPU:37, one launch (start us, length us, event | category | flops | bytes accessed | tf_op | source)
XLA Modules:
  0.0 337.8 jit_solution(9370803733377413668)
XLA Ops:
  0.0 335.9 %moe_ring.1 = bf16[32,7168]{1,0:T(8,128)(2,1)} custom-call(bf16[32,7168]{1,0:T(8,128)(2,1)} %tok_hbm.1, s32[8,32]{1,0:T(8,128)} %bitcast.2, f32[8,32]{1,0:T(8,128)} %bitcast.3, bf16[1,7168,512]{2,1,0:T(8,128)(2,1)} %gu_hbm.1, bf16[1,256,7168]{2,1,0:T(8,128)(2,1)} %dn_hbm.1), custom_call_target="tpu_custom_call" | custom-call | tf_op jit(solution)/shard_map/moe_ring/pallas_call | solution.py:288
  335.9 1.8 copy.7

commit v3 on v2

v3 whole, which is shorter than its diff:
```python
import functools

import jax
import jax.numpy as jnp
from jax import lax
from jax.experimental import pallas as pl
from jax.experimental.pallas import tpu as pltpu
from jax.sharding import PartitionSpec as P

MESH = pl.DeviceIdType.MESH
BF16 = jnp.bfloat16
F32 = jnp.float32
AHEAD, BEHIND = 0, 1


def moe_kernel(
    n, nch, top, cap,
    tok_hbm, ids_hbm, gates_hbm, gu_hbm, dn_hbm, out_hbm,
    tok, ids_in, gates_in, meta, wgu, wd, hid, hid_few, acc, part, out_buf,
    few_out, few_in, back_out, back_in,
    load_sem, out_sem, w_send, w_recv, ag_send, ag_recv, meta_send, meta_recv,
    few_send, few_recv, rs_send, rs_recv, back_send, back_recv,
):
    half = n // 2
    few = 2 * cap
    rows, width = tok.shape[2], tok.shape[3]
    inner = dn_hbm.shape[1]
    me = lax.axis_index("ep")
    core = lax.axis_index("node")
    peer = 1 - core
    ahead = lax.rem(me + 1 + core * (n - 2), n)
    behind = lax.rem(me + n - 1 - core * (n - 2), n)
    to = (ahead, behind)

    barrier = pltpu.get_barrier_semaphore()
    pl.semaphore_signal(barrier, inc=1, device_id={"ep": ahead}, device_id_type=MESH)
    pl.semaphore_signal(barrier, inc=1, device_id={"ep": behind}, device_id_type=MESH)
    pl.semaphore_signal(barrier, inc=1, device_id={"node": peer}, device_id_type=MESH)

    tok_loads = [pltpu.make_async_copy(
        tok_hbm.at[:, pl.ds(j * width, width)], tok.at[0, j], load_sem.at[j]) for j in range(nch)]
    meta_loads = [
        pltpu.make_async_copy(ids_hbm, ids_in, load_sem.at[nch]),
        pltpu.make_async_copy(gates_hbm, gates_in, load_sem.at[nch + 1]),
    ]
    for c in meta_loads + tok_loads:
        c.start()

    def gu_load(j):
        at = pl.ds(j * width, width)
        return pltpu.make_async_copy(gu_hbm.at[0, at], wgu.at[0, at], load_sem.at[nch + 2 + j])

    def gu_swap(j):
        at = pl.ds(j * width, width)
        return pltpu.make_async_remote_copy(
            src_ref=gu_hbm.at[0, at], dst_ref=wgu.at[1, at],
            send_sem=w_send.at[j], recv_sem=w_recv.at[j],
            device_id={"node": peer}, device_id_type=MESH)

    def dn_load(j):
        return pltpu.make_async_copy(
            dn_hbm.at[0, :, pl.ds(j * width, width)], wd.at[j, pl.ds(0, inner)],
            load_sem.at[2 * nch + 2 + j])

    def dn_swap(j):
        return pltpu.make_async_remote_copy(
            src_ref=dn_hbm.at[0, :, pl.ds(j * width, width)], dst_ref=wd.at[j, pl.ds(inner, inner)],
            send_sem=w_send.at[nch + j], recv_sem=w_recv.at[nch + j],
            device_id={"node": peer}, device_id_type=MESH)

    for c in meta_loads:
        c.wait()
    meta[0] = jnp.concatenate(
        [ids_in[...].astype(F32), gates_in[...], jnp.zeros((top, 128 - 2 * rows), F32)], axis=1)
    pl.semaphore_wait(barrier, 3)

    def slot(way, s):
        return s if way == AHEAD else lax.rem(n - s, n)

    def ag(way, s, j):
        return pltpu.make_async_remote_copy(
            src_ref=tok.at[slot(way, s - 1), j], dst_ref=tok.at[slot(way, s), j],
            send_sem=ag_send.at[way, j], recv_sem=ag_recv.at[way, s, j],
            device_id={"ep": to[way]}, device_id_type=MESH)

    def ag_meta(way, s):
        return pltpu.make_async_remote_copy(
            src_ref=meta.at[slot(way, s - 1)], dst_ref=meta.at[slot(way, s)],
            send_sem=meta_send.at[way], recv_sem=meta_recv.at[way, s],
            device_id={"ep": to[way]}, device_id_type=MESH)

    def ag_few(way, j):
        return pltpu.make_async_remote_copy(
            src_ref=few_out.at[way, j], dst_ref=few_in.at[way, j],
            send_sem=few_send.at[way, j], recv_sem=few_recv.at[way, j],
            device_id={"ep": to[way]}, device_id_type=MESH)

    def rs(way, d, j):
        return pltpu.make_async_remote_copy(
            src_ref=part.at[way, d, j], dst_ref=part.at[way, d - 1, j],
            send_sem=rs_send.at[way, j], recv_sem=rs_recv.at[way, d - 1, j],
            device_id={"ep": to[way]}, device_id_type=MESH)

    def rs_few(way, j):
        return pltpu.make_async_remote_copy(
            src_ref=back_out.at[way, j], dst_ref=back_in.at[way, j],
            send_sem=back_send.at[way, j], recv_sem=back_recv.at[way, j],
            device_id={"ep": to[way]}, device_id_type=MESH)

    def loop(lo, hi, body):
        def step(i, carry):
            body(i)
            return carry
        lax.fori_loop(lo, hi, step, 0)

    def matmul(x, j):
        for e in range(2):
            at = pl.ds(e * 2 * inner, 2 * inner)
            w = wgu[e, pl.ds(pl.multiple_of(j * width, width), width), :]
            acc[: x.shape[0], at] += jnp.dot(x, w, preferred_element_type=F32)

    def blocks(slots, j):
        return jnp.concatenate([tok[a, j] for a in slots], axis=0)

    lane = lax.broadcasted_iota(jnp.int32, (rows, 128), 1)
    same = lax.broadcasted_iota(jnp.int32, (rows, 128), 0) == lane
    before = (lax.broadcasted_iota(jnp.int32, (128, 128), 0)
              < lax.broadcasted_iota(jnp.int32, (128, 128), 1)).astype(F32).astype(BF16)

    def expert(chip, e):
        return (chip * 2 + (core if e == 0 else peer)).astype(F32)

    def gate_row(a, name):
        ids = meta[a]
        return jnp.sum(jnp.where(ids == name, pltpu.roll(ids, 128 - rows, 1), 0.0), axis=0, keepdims=True)

    def chosen_row(a, name):
        return jnp.sum(jnp.where(meta[a] == name, 1.0, 0.0), axis=0, keepdims=True)

    def rank_row(chosen):
        wide = jnp.broadcast_to(chosen, (8, 128)).astype(BF16)
        return jnp.dot(wide, before, preferred_element_type=F32)[0:1]

    def column(row):
        return jnp.sum(jnp.where(same, row, 0.0), axis=1, keepdims=True)

    def pick(a, chip):
        place = lax.broadcasted_iota(jnp.int32, (few, 128), 0).astype(F32)
        found = jnp.zeros((few, 128), F32)
        for e in range(2):
            chosen = chosen_row(a, expert(chip, e))
            found += jnp.where(place - e * cap == rank_row(chosen), chosen, 0.0)
        return found

    def unpick(a, chip):
        place = lane.astype(F32)
        found = jnp.zeros((rows, 128), F32)
        for e in range(2):
            chosen = chosen_row(a, expert(chip, e))
            found += jnp.where(place - e * cap == column(rank_row(chosen)), column(chosen), 0.0)
        return found[:, :few].astype(BF16)

    def gate_all(a, e):
        return column(gate_row(a, expert(me, e)))

    def gate_few(a, e):
        place = lax.broadcasted_iota(jnp.int32, (few, 128), 0).astype(F32) - e * cap
        name = expert(me, e)
        chosen = chosen_row(a, name)
        hit = jnp.where(place == rank_row(chosen), chosen * gate_row(a, name), 0.0)
        return jnp.sum(jnp.where(lax.broadcasted_iota(jnp.int32, (few, 128), 1) < rows, hit, 0.0),
                       axis=1, keepdims=True)

    def activate(slots, few_slots=()):
        count = len(slots) * rows + len(few_slots) * few
        for e in range(2):
            g = jnp.concatenate(
                [gate_all(a, e) for a in slots]
                + [gate_few(slot(way, half - way), e) for way in few_slots], axis=0)
            gate = acc[:count, pl.ds(e * 2 * inner, inner)]
            up = acc[:count, pl.ds(e * 2 * inner + inner, inner)]
            h = (gate * (1.0 / (1.0 + jnp.exp(-gate))) * up * g).astype(BF16)
            at = pl.ds(e * inner, inner)
            for i, a in enumerate(slots):
                hid[a, :, at] = h[i * rows:(i + 1) * rows]
            for i, way in enumerate(few_slots):
                first = len(slots) * rows + i * few
                hid_few[way, :, at] = h[first:first + few]
        acc[:count, :] = jnp.zeros((count, 4 * inner), F32)

    for way in (AHEAD, BEHIND):
        ag_meta(way, 1).start()
    for j in range(nch):
        tok_loads[j].wait()
        for way in (AHEAD, BEHIND):
            ag(way, 1, j).start()
    for j in range(nch):
        gu_load(j).start()
        gu_swap(j).start()
    acc[...] = jnp.zeros_like(acc)

    def arrive(copy):
        copy.wait_recv()
        copy.wait_send()

    def pass_on(s, j):
        for way in (AHEAD, BEHIND):
            arrive(ag(way, s, j))
            ag(way, s + 1, j).start()

    def pass_meta(s, ways=(AHEAD, BEHIND)):
        for way in (AHEAD, BEHIND):
            arrive(ag_meta(way, s))
            if way in ways:
                ag_meta(way, s + 1).start()

    pass_meta(1)
    loop(0, nch, lambda j: pass_on(1, j))

    opening = (0, 1, n - 1, 2, n - 2)

    def first_chunks(j):
        pass_on(2, j)
        gu_load(j).wait()
        gu_swap(j).wait_recv()
        dn_load(j).start()
        dn_swap(j).start()
        matmul(blocks(opening, j), j)

    pass_meta(2)
    loop(0, nch, first_chunks)
    activate(opening)

    def gather_step(s):
        def chunk(j):
            pass_on(s, j)
            matmul(blocks((s, n - s), j), j)
        pass_meta(s)
        loop(0, nch, chunk)
        activate((s, n - s))

    loop(3, half - 2, gather_step)

    def send_few(way, last, picked, j):
        few_out[way, j] = jnp.dot(picked, tok[last, j], preferred_element_type=F32).astype(BF16)
        ag_few(way, j).start()

    pass_meta(half - 2)
    edge_back = n - half + 2
    picked_back = pick(edge_back, behind)[:, :rows].astype(BF16)

    def back_edge(j):
        arrive(ag(AHEAD, half - 2, j))
        ag(AHEAD, half - 1, j).start()
        arrive(ag(BEHIND, half - 2, j))
        send_few(BEHIND, edge_back, picked_back, j)
        matmul(blocks((half - 2, edge_back), j), j)

    loop(0, nch, back_edge)
    activate((half - 2, edge_back))

    pass_meta(half - 1, (AHEAD,))
    edge = half - 1
    picked_ahead = pick(edge, ahead)[:, :rows].astype(BF16)

    def ahead_edge(j):
        arrive(ag(AHEAD, edge, j))
        send_few(AHEAD, edge, picked_ahead, j)
        ag_few(BEHIND, j).wait_recv()
        matmul(jnp.concatenate([tok[edge, j], few_in[BEHIND, j]], axis=0), j)

    loop(0, nch, ahead_edge)
    for j in range(nch):
        dn_load(j).wait()
        dn_swap(j).wait_recv()
    activate((edge,), (BEHIND,))

    def return_few(came):
        way = 1 - came

        def body(j):
            back_out[way, j] = jnp.dot(
                hid_few[came], wd[j], preferred_element_type=F32).astype(BF16)
            rs_few(way, j).start()
        loop(0, nch, body)

    return_few(BEHIND)

    def few_chunk(j):
        ag_few(AHEAD, j).wait_recv()
        matmul(few_in[AHEAD, j], j)

    loop(0, nch, few_chunk)
    arrive(ag_meta(AHEAD, half))
    activate((), (AHEAD,))
    return_few(AHEAD)

    def first_sums(came, d, chip):
        way = 1 - came
        a = slot(came, d)
        placed = unpick(a, chip)

        def body(j):
            mine = jnp.dot(hid[a], wd[j], preferred_element_type=F32)
            rs_few(way, j).wait_recv()
            mine += jnp.dot(placed, back_in[way, j], preferred_element_type=F32)
            part[way, d, j] = mine.astype(BF16)
            rs(way, d, j).start()
        loop(0, nch, body)

    first_sums(BEHIND, half - 2, behind)
    first_sums(AHEAD, half - 1, ahead)

    def add_part(way, d, j, own):
        rs(way, d + 1, j).wait_recv()
        part[way, d, j] = (own + part[way, d, j].astype(F32)).astype(BF16)
        rs(way, d + 1, j).wait_send()

    def reduce_step(i):
        d = half - 2 - i

        def chunk(j):
            h = jnp.concatenate([hid[n - d + 1], hid[d]], axis=0)
            mine = jnp.dot(h, wd[j], preferred_element_type=F32)
            add_part(AHEAD, d - 1, j, mine[:rows])
            add_part(BEHIND, d, j, mine[rows:])
            rs(AHEAD, d - 1, j).start()
            rs(BEHIND, d, j).start()
        loop(0, nch, chunk)

    loop(0, half - 3, reduce_step)

    def last_sums(j):
        add_part(BEHIND, 1, j, jnp.dot(hid[1], wd[j], preferred_element_type=F32))
        rs(BEHIND, 1, j).start()

    loop(0, nch, last_sums)

    def out_copy(j):
        return pltpu.make_async_copy(
            out_buf.at[j], out_hbm.at[:, pl.ds(j * width, width)], out_sem.at[j])

    for j in range(nch):
        total = jnp.dot(hid[0], wd[j], preferred_element_type=F32)
        for way in (AHEAD, BEHIND):
            arrive(rs(way, 1, j))
            total = total + part[way, 0, j].astype(F32)
        out_buf[j] = total.astype(BF16)
        out_copy(j).start()
    for j in range(nch):
        gu_swap(j).wait_send()
        dn_swap(j).wait_send()
        for way in (AHEAD, BEHIND):
            ag_few(way, j).wait_send()
            rs_few(way, j).wait_send()
        out_copy(j).wait()


def on_device(n, tokens, expert_ids, gate_weights, gate_up_weight, down_weight):
    rows, model = tokens.shape
    top = expert_ids.shape[1]
    inner = down_weight.shape[1]
    experts = 2 * n
    cap = 2 * rows * top // experts
    few = 2 * cap
    nch = 4
    width = model // nch
    half = n // 2
    dma = pltpu.SemaphoreType.DMA
    hbm = pl.BlockSpec(memory_space=pl.ANY)
    return pl.pallas_call(
        functools.partial(moe_kernel, n, nch, top, cap),
        out_shape=jax.ShapeDtypeStruct((rows, model), BF16),
        in_specs=[hbm] * 5,
        out_specs=hbm,
        scratch_shapes=[
            pltpu.VMEM((n, nch, rows, width), BF16),
            pltpu.VMEM((top, rows), jnp.int32),
            pltpu.VMEM((top, rows), F32),
            pltpu.VMEM((n, top, 128), F32),
            pltpu.VMEM((2, model, 2 * inner), BF16),
            pltpu.VMEM((nch, 2 * inner, width), BF16),
            pltpu.VMEM((n, rows, 2 * inner), BF16),
            pltpu.VMEM((2, few, 2 * inner), BF16),
            pltpu.VMEM((5 * rows, 4 * inner), F32),
            pltpu.VMEM((2, half, nch, rows, width), BF16),
            pltpu.VMEM((nch, rows, width), BF16),
            pltpu.VMEM((2, nch, few, width), BF16),
            pltpu.VMEM((2, nch, few, width), BF16),
            pltpu.VMEM((2, nch, few, width), BF16),
            pltpu.VMEM((2, nch, few, width), BF16),
            dma((3 * nch + 2,)),
            dma((nch,)),
            dma((2 * nch,)),
            dma((2 * nch,)),
            dma((2, nch)),
            dma((2, half, nch)),
            dma((2,)),
            dma((2, half + 1)),
            dma((2, nch)),
            dma((2, nch)),
            dma((2, nch)),
            dma((2, half, nch)),
            dma((2, nch)),
            dma((2, nch)),
        ],
        compiler_params=pltpu.CompilerParams(
            collective_id=0, has_side_effects=True, vmem_limit_bytes=66_000_000),
        name="moe_ring",
    )(tokens, expert_ids.T, gate_weights.T, gate_up_weight, down_weight)


def solution(mesh):
    placed = (
        P(("groups", "ep", "node"), None),
        P(("groups", "ep", "node"), None),
        P(("groups", "ep", "node"), None),
        P(("ep", "node"), None, None),
        P(("ep", "node"), None, None),
    )
    return jax.shard_map(
        functools.partial(on_device, mesh.shape["ep"]),
        mesh=mesh,
        in_specs=placed,
        out_specs=P(("groups", "ep", "node"), None),
        check_vma=False,
    )
```

time: 338 us -> 331 us (0.979)
  Pallas kernels: 336 us -> 329 us
    pallas_call x1, Pallas kernels: 336 us -> 329 us  [on_device(): pl.pallas_call(functools.partial(moe_kernel, n, nch, top, cap), out_shape...]
where the time goes in v3:
time: 331 us
  Pallas kernels  329 us (99%)
    pallas_call x1, Pallas kernels, on_device(): pl.pallas_call(functools.partial(moe_kernel, n, nch, top, cap), out_shape...  329 us

profile of v3, /device:TPU:37, one launch (start us, length us, event | category | flops | bytes accessed | tf_op | source)
XLA Modules:
  0.0 330.9 jit_solution(7274009737418187325)
XLA Ops:
  0.0 329.1 %moe_ring.1 = bf16[32,7168]{1,0:T(8,128)(2,1)} custom-call(bf16[32,7168]{1,0:T(8,128)(2,1)} %tok_hbm.1, s32[8,32]{1,0:T(8,128)} %bitcast.2, f32[8,32]{1,0:T(8,128)} %bitcast.3, bf16[1,7168,512]{2,1,0:T(8,128)(2,1)} %gu_hbm.1, bf16[1,256,7168]{2,1,0:T(8,128)(2,1)} %dn_hbm.1), custom_call_target="tpu_custom_call" | custom-call | tf_op jit(solution)/shard_map/moe_ring/pallas_call | solution.py:371
  329.1 1.8 copy.7

commit v4 on v3

--- a/solution.py
+++ b/solution.py
@@ -70,8 +70,10 @@
 
     for c in meta_loads:
         c.wait()
+    coarse = gates_in[...].astype(BF16).astype(F32)
     meta[0] = jnp.concatenate(
-        [ids_in[...].astype(F32), gates_in[...], jnp.zeros((top, 128 - 2 * rows), F32)], axis=1)
+        [ids_in[...].astype(F32), coarse, gates_in[...] - coarse,
+         jnp.zeros((top, 128 - 3 * rows), F32)], axis=1).astype(BF16)
     pl.semaphore_wait(barrier, 3)
 
     def slot(way, s):
@@ -131,11 +133,12 @@
         return (chip * 2 + (core if e == 0 else peer)).astype(F32)
 
     def gate_row(a, name):
-        ids = meta[a]
-        return jnp.sum(jnp.where(ids == name, pltpu.roll(ids, 128 - rows, 1), 0.0), axis=0, keepdims=True)
+        ids = meta[a].astype(F32)
+        gates = pltpu.roll(ids, 128 - rows, 1) + pltpu.roll(ids, 128 - 2 * rows, 1)
+        return jnp.sum(jnp.where(ids == name, gates, 0.0), axis=0, keepdims=True)
 
     def chosen_row(a, name):
-        return jnp.sum(jnp.where(meta[a] == name, 1.0, 0.0), axis=0, keepdims=True)
+        return jnp.sum(jnp.where(meta[a].astype(F32) == name, 1.0, 0.0), axis=0, keepdims=True)
 
     def rank_row(chosen):
         wide = jnp.broadcast_to(chosen, (8, 128)).astype(BF16)
@@ -284,17 +287,6 @@
             rs_few(way, j).start()
         loop(0, nch, body)
 
-    return_few(BEHIND)
-
-    def few_chunk(j):
-        ag_few(AHEAD, j).wait_recv()
-        matmul(few_in[AHEAD, j], j)
-
-    loop(0, nch, few_chunk)
-    arrive(ag_meta(AHEAD, half))
-    activate((), (AHEAD,))
-    return_few(AHEAD)
-
     def first_sums(came, d, chip):
         way = 1 - came
         a = slot(came, d)
@@ -308,7 +300,17 @@
             rs(way, d, j).start()
         loop(0, nch, body)
 
+    return_few(BEHIND)
     first_sums(BEHIND, half - 2, behind)
+
+    def few_chunk(j):
+        ag_few(AHEAD, j).wait_recv()
+        matmul(few_in[AHEAD, j], j)
+
+    loop(0, nch, few_chunk)
+    arrive(ag_meta(AHEAD, half))
+    activate((), (AHEAD,))
+    return_few(AHEAD)
     first_sums(AHEAD, half - 1, ahead)
 
     def add_part(way, d, j, own):
@@ -377,7 +379,7 @@
             pltpu.VMEM((n, nch, rows, width), BF16),
             pltpu.VMEM((top, rows), jnp.int32),
             pltpu.VMEM((top, rows), F32),
-            pltpu.VMEM((n, top, 128), F32),
+            pltpu.VMEM((n, top, 128), BF16),
             pltpu.VMEM((2, model, 2 * inner), BF16),
             pltpu.VMEM((nch, 2 * inner, width), BF16),
             pltpu.VMEM((n, rows, 2 * inner), BF16),

time: 331 us -> 330 us (level)
  no operation moved by 1% of the time
where the time goes in v4:
time: 330 us
  Pallas kernels  329 us (100%)
    pallas_call x1, Pallas kernels, on_device(): pl.pallas_call(functools.partial(moe_kernel, n, nch, top, cap), out_shape...  329 us

profile of v4, /device:TPU:37, one launch (start us, length us, event | category | flops | bytes accessed | tf_op | source)
XLA Modules:
  0.0 330.3 jit_solution(5572143498401829094)
XLA Ops:
  0.0 328.5 %moe_ring.1 = bf16[32,7168]{1,0:T(8,128)(2,1)} custom-call(bf16[32,7168]{1,0:T(8,128)(2,1)} %tok_hbm.1, s32[8,32]{1,0:T(8,128)} %bitcast.2, f32[8,32]{1,0:T(8,128)} %bitcast.3, bf16[1,7168,512]{2,1,0:T(8,128)(2,1)} %gu_hbm.1, bf16[1,256,7168]{2,1,0:T(8,128)(2,1)} %dn_hbm.1), custom_call_target="tpu_custom_call" | custom-call | tf_op jit(solution)/shard_map/moe_ring/pallas_call | solution.py:373
  328.5 1.8 copy.7

commit v5 on v4

--- a/solution.py
+++ b/solution.py
@@ -265,6 +265,7 @@
     pass_meta(half - 1, (AHEAD,))
     edge = half - 1
     picked_ahead = pick(edge, ahead)[:, :rows].astype(BF16)
+    placed = (unpick(edge, ahead), unpick(edge_back, behind))
 
     def ahead_edge(j):
         arrive(ag(AHEAD, edge, j))
@@ -287,21 +288,19 @@
             rs_few(way, j).start()
         loop(0, nch, body)
 
-    def first_sums(came, d, chip):
+    def first_sums(came, d):
         way = 1 - came
         a = slot(came, d)
-        placed = unpick(a, chip)
 
         def body(j):
             mine = jnp.dot(hid[a], wd[j], preferred_element_type=F32)
             rs_few(way, j).wait_recv()
-            mine += jnp.dot(placed, back_in[way, j], preferred_element_type=F32)
+            mine += jnp.dot(placed[came], back_in[way, j], preferred_element_type=F32)
             part[way, d, j] = mine.astype(BF16)
             rs(way, d, j).start()
         loop(0, nch, body)
 
     return_few(BEHIND)
-    first_sums(BEHIND, half - 2, behind)
 
     def few_chunk(j):
         ag_few(AHEAD, j).wait_recv()
@@ -311,7 +310,8 @@
     arrive(ag_meta(AHEAD, half))
     activate((), (AHEAD,))
     return_few(AHEAD)
-    first_sums(AHEAD, half - 1, ahead)
+    first_sums(BEHIND, half - 2)
+    first_sums(AHEAD, half - 1)
 
     def add_part(way, d, j, own):
         rs(way, d + 1, j).wait_recv()

time: 330 us -> 330 us (level)
  no operation moved by 1% of the time
where the time goes in v5:
time: 330 us
  Pallas kernels  328 us (99%)
    pallas_call x1, Pallas kernels, on_device(): pl.pallas_call(functools.partial(moe_kernel, n, nch, top, cap), out_shape...  328 us

profile of v5, /device:TPU:37, one launch (start us, length us, event | category | flops | bytes accessed | tf_op | source)
XLA Modules:
  0.0 330.2 jit_solution(9776841841378986658)
XLA Ops:
  0.0 328.4 %moe_ring.1 = bf16[32,7168]{1,0:T(8,128)(2,1)} custom-call(bf16[32,7168]{1,0:T(8,128)(2,1)} %tok_hbm.1, s32[8,32]{1,0:T(8,128)} %bitcast.2, f32[8,32]{1,0:T(8,128)} %bitcast.3, bf16[1,7168,512]{2,1,0:T(8,128)(2,1)} %gu_hbm.1, bf16[1,256,7168]{2,1,0:T(8,128)(2,1)} %dn_hbm.1), custom_call_target="tpu_custom_call" | custom-call | tf_op jit(solution)/shard_map/moe_ring/pallas_call | solution.py:373
  328.4 1.8 copy.7
